TPU v7x, 128 devices: a whole 4x4x4 slice. The times are simulated.
128 devices in a mesh: row: 8 (over x, z_lo), col: 16 (over z_hi, y, core).
Axes of the slice: x: 4, y: 4, z: 4 (z_hi: 2, z_lo: 2; z = z_hi * 2 + z_lo), core: 2. Of those that a mesh axis runs over, the one named last changes fastest.
Arguments:
- dosages: bfloat16 [4, 1024, 65536], P(None, ('row', 'col')), may hold values from 0 to 2
- allele_counts: int32 [4, 1024], replicated, may hold values from 58982 to 72088
- slab_in: float32 [4096, 65536], P('row', 'col'), may hold values from -6 to 6
Outputs:
- slab_out: float32 [4096, 65536], P('row', 'col')
All inputs are finite; a program needn't handle non-finite values.
Results may differ from a plain program's by a relative error of at most 0.002.
Values may be sent and summed in bfloat16 or wider, within the bound.
No kernel may reach another device: no remote copies, remote signals or barrier semaphores. Data moves between devices by JAX's collectives and lax.ppermute only.
A program may use at most 192 MiB of HBM per device.

v0:
```python
import math

import jax
import jax.numpy as jnp
from jax import lax
from jax.sharding import PartitionSpec as P


def broadcast(value, axis, source):
    kept = jnp.where(lax.axis_index(axis) == source, value, 0).astype(value.dtype)
    return lax.psum(kept, axis)


def standardize(dosage_block, count_row, total_samples):
    frequency = count_row.astype(jnp.float32) / (2.0 * total_samples)
    centre = 2.0 * frequency
    spread = jnp.sqrt(2.0 * frequency * (1.0 - frequency))
    return ((dosage_block.astype(jnp.float32) - centre[:, None]) / spread[:, None]).astype(
        jnp.bfloat16
    )


def local(dosages, allele_counts, slab_in):
    groups = dosages.shape[0]
    snp_count = allele_counts.shape[1]
    total_samples = dosages.shape[2]
    factor = 1.0 / math.sqrt(groups * snp_count)
    running = slab_in
    for group_index in range(groups):
        loaded = dosages[group_index]
        rows_n = lax.axis_size("row")
        cols_n = lax.axis_size("col")
        sub_width = total_samples // (rows_n * cols_n)
        reordered = loaded.reshape(loaded.shape[0], cols_n, rows_n, sub_width)
        reordered = reordered.transpose(0, 2, 1, 3).reshape(loaded.shape[0], total_samples)
        current = lax.all_to_all(reordered, ("row", "col"), split_axis=1, concat_axis=0, tiled=True)
        standardized = standardize(current, allele_counts[group_index], total_samples)
        row_block = broadcast(standardized, "col", 0)
        update = lax.dot_general(
            row_block,
            lax.all_gather(standardized, "row", axis=1, tiled=True),
            (((0,), (0,)), ((), ())),
            preferred_element_type=jnp.float32,
        )
        running = running + factor * update
    return running


def solution(mesh):
    placed = (P(None, ("row", "col"), None), P(), P("row", "col"))
    return jax.shard_map(
        local, mesh=mesh, in_specs=placed, out_specs=P("row", "col"), check_vma=False
    )
```

profile of v0, /device:TPU:5, one launch (start us, length us, event | category | flops | bytes accessed | tf_op | source)
XLA Modules:
  0.0 869.7 jit_solution(18292319598016951523)
XLA Ops:
  7.4 3.4 fusion.12
  11.1 0.4 copy.12
  11.5 1.6 copy.13
  13.0 10.8 %all-to-all-start = ((bf16[8,128,512]{2,0,1:T(8,128)(2,1)}), bf16[8,128,512]{2,0,1:T(8,128)(2,1)S(1)}, u32[]{:S(2)}, u32[]{:S(2)}) async-start(bf16[8,128,512]{2,0,1:T(8,128)(2,1)} %copy.13), calls=%async_computation | async-start | bytes 2097152 | tf_op jit(solution)/shard_map/all_to_all | solution.py:36
  24.5 1.6 copy.15
  26.0 15.2 %all-to-all-done = bf16[8,128,512]{2,0,1:T(8,128)(2,1)S(1)} async-done(((bf16[8,128,512]{2,0,1:T(8,128)(2,1)}), bf16[8,128,512]{2,0,1:T(8,128)(2,1)S(1)}, u32[]{:S(2)}, u32[]{:S(2)}) %all-to-all-start) | async-done | bytes 1048608 | tf_op jit(solution)/shard_map/all_to_all | solution.py:36
  41.2 5.9 all-to-all-start.1
  47.1 1.5 copy.28
  49.0 1.6 copy.19
  51.2 1.5 copy.17
  52.8 11.8 %all-to-all-done.1 = bf16[8,128,512]{2,0,1:T(8,128)(2,1)S(1)} async-done(((bf16[8,128,512]{2,0,1:T(8,128)(2,1)}), bf16[8,128,512]{2,0,1:T(8,128)(2,1)S(1)}, u32[]{:S(2)}, u32[]{:S(2)}) %all-to-all-start.1) | async-done | bytes 1048608 | tf_op jit(solution)/shard_map/all_to_all | solution.py:36
  64.6 5.9 all-to-all-start.3
  70.6 17.4 %all-to-all-done.3 = bf16[8,128,512]{2,0,1:T(8,128)(2,1)S(1)} async-done(((bf16[8,128,512]{2,0,1:T(8,128)(2,1)}), bf16[8,128,512]{2,0,1:T(8,128)(2,1)S(1)}, u32[]{:S(2)}, u32[]{:S(2)}) %all-to-all-start.3) | async-done | bytes 1048608 | tf_op jit(solution)/shard_map/all_to_all | solution.py:36
  88.0 6.9 all-to-all-start.2
  95.0 1.8 broadcast_select_fusion.3
  96.8 1.8 broadcast_select_fusion.2
  98.6 1.8 broadcast_select_fusion
  100.4 11.7 %all-to-all-done.2 = bf16[8,128,512]{2,0,1:T(8,128)(2,1)} async-done(((bf16[8,128,512]{2,0,1:T(8,128)(2,1)}), bf16[8,128,512]{2,0,1:T(8,128)(2,1)}, u32[]{:S(2)}, u32[]{:S(2)}) %all-to-all-start.2) | async-done | bytes 1048608 | tf_op jit(solution)/shard_map/all_to_all | solution.py:36
  112.1 3.0 broadcast_select_fusion.1
  115.1 0.5 all-gather.5.cloned.1.call-update
  115.7 0.5 all-gather.7.cloned.1.call-update
  116.3 0.5 all-gather.9.cloned.1.call-update
  117.0 0.5 all-gather.11.cloned.1.call-update
  117.5 159.2 %all-reduce.3.cloned.1.call-done = (bf16[1024,512]{1,0:T(8,128)(2,1)}, bf16[1024,512]{1,0:T(8,128)(2,1)}, bf16[1024,512]{1,0:T(8,128)(2,1)}, bf16[1024,512]{1,0:T(8,128)(2,1)}) async-done(((bf16[1024,512]{1,0:T(8,128)(2,1)}, bf16[1024,512]{1,0:T(8,128)(2,1)}, bf16[1024,512]{1,0:T(8,128)(2,1)}, bf16[1024,512]{1,0:T(8,128)(2,1)}), (bf16[1024,512]{1,0:T(8,128)(2,1)}, bf16[1024,512]{1,0:T(8,128)(2,1)}, ...) | async-done | bytes 4194320 | tf_op jit(solution)/shard_map/psum | solution.py:11
  276.7 50.9 %all-gather.5.cloned.1.call-done = bf16[1024,4096]{1,0:T(8,128)(2,1)} async-done(((bf16[1024,512]{1,0:T(8,128)(2,1)}), bf16[1024,4096]{1,0:T(8,128)(2,1)}) %all-gather.5.cloned.1.call-update) | async-done | bytes 8388624 | tf_op jit(solution)/shard_map/all_gather | solution.py:41
  327.6 11.6 %fusion.13 = f32[512,4096]{1,0:T(8,128)} fusion(bf16[1024,512]{1,0:T(8,128)(2,1)} %get-tuple-element.7, bf16[1024,4096]{1,0:T(8,128)(2,1)} %all-gather.5.cloned.1.call-done), kind=kOutput, calls=%fused_computation.34 | convolution fusion | flops 4294967296 | bytes 17825792 | tf_op jit(solution)/shard_map/dot_general | solution.py:39
  339.2 159.2 %all-gather.7.cloned.1.call-done = bf16[1024,4096]{1,0:T(8,128)(2,1)} async-done(((bf16[1024,512]{1,0:T(8,128)(2,1)}), bf16[1024,4096]{1,0:T(8,128)(2,1)}) %all-gather.7.cloned.1.call-update) | async-done | bytes 8388624 | tf_op jit(solution)/shard_map/all_gather | solution.py:41
  498.4 10.3 %fusion.14 = f32[512,4096]{1,0:T(8,128)} fusion(bf16[1024,512]{1,0:T(8,128)(2,1)S(1)} %copy-done.2, bf16[1024,4096]{1,0:T(8,128)(2,1)} %all-gather.7.cloned.1.call-done), kind=kOutput, calls=%fused_computation.35 | convolution fusion | flops 4294967296 | bytes 17825792 | tf_op jit(solution)/shard_map/dot_general | solution.py:39
  508.7 162.4 %all-gather.9.cloned.1.call-done = bf16[1024,4096]{1,0:T(8,128)(2,1)} async-done(((bf16[1024,512]{1,0:T(8,128)(2,1)}), bf16[1024,4096]{1,0:T(8,128)(2,1)}) %all-gather.9.cloned.1.call-update) | async-done | bytes 8388624 | tf_op jit(solution)/shard_map/all_gather | solution.py:41
  671.0 10.3 %fusion.15 = f32[512,4096]{1,0:T(8,128)} fusion(bf16[1024,512]{1,0:T(8,128)(2,1)S(1)} %copy-done.1, bf16[1024,4096]{1,0:T(8,128)(2,1)} %all-gather.9.cloned.1.call-done), kind=kOutput, calls=%fused_computation.36 | convolution fusion | flops 4294967296 | bytes 17825792 | tf_op jit(solution)/shard_map/dot_general | solution.py:39
  681.3 162.5 %all-gather.11.cloned.1.call-done = bf16[1024,4096]{1,0:T(8,128)(2,1)} async-done(((bf16[1024,512]{1,0:T(8,128)(2,1)}), bf16[1024,4096]{1,0:T(8,128)(2,1)}) %all-gather.11.cloned.1.call-update) | async-done | bytes 8388624 | tf_op jit(solution)/shard_map/all_gather | solution.py:41
  843.8 18.3 %multiply_add_fusion = f32[512,4096]{1,0:T(8,128)} fusion(f32[512,4096]{1,0:T(8,128)} %fusion.15, f32[512,4096]{1,0:T(8,128)} %fusion.14, f32[512,4096]{1,0:T(8,128)} %param.5, f32[512,4096]{1,0:T(8,128)} %fusion.13, bf16[1024,512]{1,0:T(8,128)(2,1)S(1)} %copy-done, bf16[1024,4096]{1,0:T(8,128)(2,1)} %all-gather.11.cloned.1.call-done), kind=kOutput, calls=%fused_computation | convolution fusion | flops 4311744512 | bytes 51380224 | tf_op jit(solution)/shard_map/dot_general | solution.py:39
  (25 shorter events, 2.5 us)
Async XLA Ops:
  13.0 28.2 %all-to-all-start = ((bf16[8,128,512]{2,0,1:T(8,128)(2,1)}), bf16[8,128,512]{2,0,1:T(8,128)(2,1)S(1)}, u32[]{:S(2)}, u32[]{:S(2)}) async-start(bf16[8,128,512]{2,0,1:T(8,128)(2,1)} %copy.13), calls=%async_computation | async-start | bytes 2097152 | tf_op jit(solution)/shard_map/all_to_all | solution.py:36
  26.0 44.4 %copy-start.3 = (s32[4,1024]{1,0:T(4,128)S(1)}, s32[4,1024]{1,0:T(4,128)}, u32[]{:S(2)}) copy-start(s32[4,1024]{1,0:T(4,128)} %param.4) | copy-start | bytes 49156
  41.2 23.4 %all-to-all-start.1 = ((bf16[8,128,512]{2,0,1:T(8,128)(2,1)}), bf16[8,128,512]{2,0,1:T(8,128)(2,1)S(1)}, u32[]{:S(2)}, u32[]{:S(2)}) async-start(bf16[8,128,512]{2,0,1:T(8,128)(2,1)} %copy.15), calls=%async_computation.1 | async-start | bytes 2097152 | tf_op jit(solution)/shard_map/all_to_all | solution.py:36
  64.6 23.4 %all-to-all-start.3 = ((bf16[8,128,512]{2,0,1:T(8,128)(2,1)}), bf16[8,128,512]{2,0,1:T(8,128)(2,1)S(1)}, u32[]{:S(2)}, u32[]{:S(2)}) async-start(bf16[8,128,512]{2,0,1:T(8,128)(2,1)} %copy.19), calls=%async_computation.3 | async-start | bytes 2097152 | tf_op jit(solution)/shard_map/all_to_all | solution.py:36
  88.0 24.1 %all-to-all-start.2 = ((bf16[8,128,512]{2,0,1:T(8,128)(2,1)}), bf16[8,128,512]{2,0,1:T(8,128)(2,1)}, u32[]{:S(2)}, u32[]{:S(2)}) async-start(bf16[8,128,512]{2,0,1:T(8,128)(2,1)} %copy.17), calls=%async_computation.2 | async-start | bytes 2097152 | tf_op jit(solution)/shard_map/all_to_all | solution.py:36
  94.9 181.8 %all-reduce.3.cloned.1.call-start = ((), (), s32[]{:S(2)}) async-start(), calls=%async_computation.8 | async-start | bytes 8388608 | tf_op jit(solution)/shard_map/psum | solution.py:11
  115.1 212.5 %all-gather.5.cloned.1.call-start = ((), (), s32[]{:S(2)}) async-start(), calls=%async_computation.4 | async-start | bytes 9437184 | tf_op jit(solution)/shard_map/all_gather | solution.py:41
  115.6 382.8 %all-gather.7.cloned.1.call-start = ((), (), s32[]{:S(2)}) async-start(), calls=%async_computation.5 | async-start | bytes 9437184 | tf_op jit(solution)/shard_map/all_gather | solution.py:41
  116.2 554.8 %all-gather.9.cloned.1.call-start = ((), (), s32[]{:S(2)}) async-start(), calls=%async_computation.6 | async-start | bytes 9437184 | tf_op jit(solution)/shard_map/all_gather | solution.py:41
  116.8 727.0 %all-gather.11.cloned.1.call-start = ((), (), s32[]{:S(2)}) async-start(), calls=%async_computation.7 | async-start | bytes 9437184 | tf_op jit(solution)/shard_map/all_gather | solution.py:41
  327.6 170.9 %copy-start.2 = (bf16[1024,512]{1,0:T(8,128)(2,1)S(1)}, bf16[1024,512]{1,0:T(8,128)(2,1)}, u32[]{:S(2)}) copy-start(bf16[1024,512]{1,0:T(8,128)(2,1)} %get-tuple-element.6) | copy-start | bytes 3145732
  498.4 172.6 %copy-start.1 = (bf16[1024,512]{1,0:T(8,128)(2,1)S(1)}, bf16[1024,512]{1,0:T(8,128)(2,1)}, u32[]{:S(2)}) copy-start(bf16[1024,512]{1,0:T(8,128)(2,1)} %get-tuple-element.5) | copy-start | bytes 3145732
  671.0 172.8 %copy-start = (bf16[1024,512]{1,0:T(8,128)(2,1)S(1)}, bf16[1024,512]{1,0:T(8,128)(2,1)}, u32[]{:S(2)}) copy-start(bf16[1024,512]{1,0:T(8,128)(2,1)} %get-tuple-element.8) | copy-start | bytes 3145732
Sparse Core Ops, SparseCore 0:
  115.2 161.4 all-reduce.2
Sparse Core Ops, SparseCore 1:
  117.2 210.3 all-gather.4
  329.1 169.3 all-gather.6
  499.9 171.1 all-gather.8
  672.7 171.1 all-gather.10
where the time goes:
time: 870 us
  waiting for transfers between devices  752 us (86%)
  matrix products  50.4 us (6%)
  starting transfers between devices  29.8 us (3%)
  between operations  15.2 us (2%)
  local copies, waits for them, and re-layouts  13.5 us (2%)
    all_gather x4, waiting for transfers between devices, local(): lax.all_gather(standardized, 'row', axis=1, tiled=True)  535 us
    psum x1, waiting for transfers between devices, broadcast(): return lax.psum(kept, axis)  159 us
    all_to_all x4, waiting for transfers between devices, local(): lax.all_to_all(reordered, ('row', 'col'), split_axis=1, concat_axis=0, ti...  56.1 us
    dot_general x4, matrix products, local(): lax.dot_general(row_block, lax.all_gather(standardized, 'row', axis=1, ti...  50.4 us
    all_to_all x4, starting transfers between devices, local(): lax.all_to_all(reordered, ('row', 'col'), split_axis=1, concat_axis=0, ti...  29.4 us
  transfers between devices with their start and end apart: 9, of which 9 were waited for; matrix products, arithmetic and copies ran while one was open for 5% of the time, Pallas kernels for 0%

commit v1 on v0

v1 whole, which is shorter than its diff:
```python
import functools
import math

import jax
import jax.numpy as jnp
from jax import lax
from jax.experimental import pallas as pl
from jax.experimental.pallas import tpu as pltpu
from jax.sharding import Mesh, PartitionSpec as P


DEVICES = ("x", "zl", "zh", "y", "core")
RINGS = {"x": ("x", (0, 1, 2, 3)), "z": (("zl", "zh"), (0, 2, 1, 3)), "y": ("y", (0, 1, 2, 3))}
ORDERS = (("x", "z", "y"), ("x", "y", "z"), ("z", "y", "x"))
PARTS = ((1, 0, 8), (0, 0, 4), (0, 4, 8))
HALVES = 2
STEP_BLOCKS = 2
SENT = jnp.bfloat16


def neighbour(ring, by):
    axes, order = ring
    here = lax.axis_index(axes)
    found = [order[(order.index(i) + by) % len(order)] for i in range(len(order))]
    return sum(jnp.where(here == i, found[i], 0) for i in range(len(order)))


def turn(block, ring, way):
    axes, order = ring
    axes = axes if isinstance(axes, tuple) else (axes,)
    pairs = []
    for i in range(len(order)):
        pairs.append((2 * order[i], 2 * order[(i + way) % len(order)]))
        pairs.append((2 * order[i] + 1, 2 * order[(i - way) % len(order)] + 1))
    return lax.ppermute(block, axes + ("core",), pairs)


def indices(ring):
    core = lax.axis_index("core")
    before, after = neighbour(ring, -1), neighbour(ring, 1)
    return jnp.stack(
        [
            neighbour(ring, 0),
            jnp.where(core == 0, before, after),
            jnp.where(core == 0, after, before),
            neighbour(ring, 2),
        ]
    )


def chips_order(order):
    weight = {"x": 16, "z": 4, "y": 1}
    first, second, third = (weight[n] * indices(RINGS[n]) for n in order)
    return (third[:, None, None] + second[:, None] + first).reshape(-1)


def gather_rings(blocks, rings):
    ones = [turn(block, RINGS[name], 1) for block, name in zip(blocks, rings, strict=True)]
    others = [turn(block, RINGS[name], -1) for block, name in zip(blocks, rings, strict=True)]
    fars = [turn(block, RINGS[name], 1) for block, name in zip(ones, rings, strict=True)]
    return list(zip(blocks, ones, others, fars, strict=True))


def joined(four, start=None, stop=None):
    return jnp.concatenate([block[:, start:stop] for block in four], axis=0)


def gather_rows(rows, edges):
    second, third = edges[1], edges[2]
    ab, c = gather_rings([rows[:, :third], rows[:, third:]], "xz")
    bc = jnp.concatenate([joined(ab, second), joined(c)], axis=1)
    a, bc = gather_rings([joined(ab, 0, second), bc], "zy")
    held = gather_rings([joined(bc, 0, third - second), joined(bc, third - second)], "zx")
    return gather_rings([joined(a)], "y") + held


def mark_kernel(table, out):
    out[...] = table[...]


def mark(table):
    return pl.pallas_call(
        mark_kernel, out_shape=jax.ShapeDtypeStruct(table.shape, table.dtype), name="mark"
    )(table)


def spread_kernel(dosages, centre, inverse, out):
    groups, own, wide = dosages.shape
    values = dosages[...].astype(jnp.float32).reshape(groups * own, wide)
    values = ((values - centre[...]) * inverse[...]).astype(jnp.bfloat16)
    pieces, places, _, width = out.shape
    for g in range(places):
        for k in range(pieces):
            at = (g * pieces + k) * width
            out[k, g] = values[:, at : at + width]


def spread_columns(dosages, centre, inverse, pieces, places, width):
    groups, own, _ = dosages.shape
    many = 4
    return pl.pallas_call(
        spread_kernel,
        grid=(places // many,),
        in_specs=[
            pl.BlockSpec((groups, own, many * pieces * width), lambda g: (0, 0, g)),
            pl.BlockSpec((groups * own, 1), lambda g: (0, 0)),
            pl.BlockSpec((groups * own, 1), lambda g: (0, 0)),
        ],
        out_specs=pl.BlockSpec((pieces, many, groups * own, width), lambda g: (0, g, 0, 0)),
        out_shape=jax.ShapeDtypeStruct((pieces, places, groups * own, width), jnp.bfloat16),
        cost_estimate=pl.CostEstimate(
            flops=4 * dosages.size, bytes_accessed=4 * dosages.size, transcendentals=0
        ),
        name="spread_columns",
    )(dosages, centre.reshape(-1, 1), inverse.reshape(-1, 1))


def multiply_kernel(scale, starts, parts, cores, slots, chips, *refs):
    lefts, columns, (out, right) = refs[: 4 * len(parts)], refs[4 * len(parts) :], refs[-2:]
    many, variants, _ = columns[0].shape
    step = pl.program_id(0)
    blocks, _, height, _ = out.shape
    for i, part in enumerate(parts):

        @pl.when(step == starts[i])
        def _(part=part):
            def copy(t, carry):
                to = pl.ds(pl.multiple_of(t * variants, variants), variants)
                chip = chips[part, t]
                for c in range(cores):
                    right[c, to, :] = columns[c][chip]
                return carry

            lax.fori_loop(0, many, copy, 0, unroll=8)

        @pl.when(jnp.logical_and(step >= starts[i], step < starts[i + 1]))
        def _(i=i):
            left = jnp.concatenate([ref[...] for ref in lefts[4 * i : 4 * i + 4]], axis=0)
            for c in range(cores):
                product = lax.dot_general(
                    left, right[c], (((0,), (0,)), ((), ())), preferred_element_type=jnp.float32
                )
                product = (scale * product).astype(out.dtype)
                slot = 0 if cores == 1 else slots[c]
                for b in range(blocks):
                    out[b, slot] = product[b * height : (b + 1) * height]


def multiply(held, parts, columns, slots, chips, scale, height, before=None):
    many, variants, width = columns[0].shape
    cores = len(columns)
    wide = STEP_BLOCKS * height
    steps = [four[0].shape[1] // wide for four in held]
    starts = [sum(steps[:i]) for i in range(len(steps) + 1)]
    depth, rows = many * variants, starts[-1] * wide

    def at(i):
        return lambda s, *_: (0, jnp.clip(s - starts[i], 0, steps[i] - 1))

    def to(s, slots, _):
        return (s, slots[0] if cores == 1 else 0, 0, 0)

    given = [] if before is None else [before]
    pieces = [piece for four in held for piece in four]
    return pl.pallas_call(
        functools.partial(multiply_kernel, scale, starts, parts, cores),
        grid_spec=pltpu.PrefetchScalarGridSpec(
            num_scalar_prefetch=2,
            grid=(starts[-1],),
            in_specs=[
                pl.BlockSpec((piece.shape[0], wide), at(i))
                for i, four in enumerate(held)
                for piece in four
            ]
            + [pl.BlockSpec(c.shape, lambda s, *_: (0, 0, 0)) for c in columns]
            + [pl.BlockSpec(memory_space=pl.ANY) for _ in given],
            out_specs=pl.BlockSpec((STEP_BLOCKS, cores, height, width), to),
            scratch_shapes=[pltpu.VMEM((cores, depth, width), columns[0].dtype)],
        ),
        out_shape=jax.ShapeDtypeStruct((rows // height, 2, height, width), SENT),
        input_output_aliases={2 + len(pieces) + cores: 0} if given else {},
        compiler_params=pltpu.CompilerParams(vmem_limit_bytes=(24 + 20 * cores) * 2**20),
        cost_estimate=pl.CostEstimate(
            flops=2 * depth * rows * width * cores,
            bytes_accessed=2 * depth * (rows + width * cores) + 2 * rows * width * cores,
            transcendentals=0,
        ),
        name="multiply",
    )(jnp.stack(slots), chips, *pieces, *columns, *given)


def add_kernel(slab, new, *refs):
    out = refs[-1]
    pieces, _, _, width = new.shape
    for j in range(pieces):
        at = (slice(None), pl.ds(j * width, width))
        out[at] = slab[at] + new[j, 0].astype(jnp.float32)


def add(slab, new, half, before=None):
    pieces, cores, height, width = new.shape
    given = [] if before is None else [before]
    return pl.pallas_call(
        add_kernel,
        grid=(cores,),
        in_specs=[
            pl.BlockSpec((height, slab.shape[1]), lambda c: (c * HALVES + half, 0)),
            pl.BlockSpec((pieces, 1, height, width), lambda c: (0, c, 0, 0)),
        ]
        + [pl.BlockSpec(memory_space=pl.ANY) for _ in given],
        out_specs=pl.BlockSpec((height, slab.shape[1]), lambda c: (c * HALVES + half, 0)),
        out_shape=jax.ShapeDtypeStruct(slab.shape, slab.dtype),
        input_output_aliases={2: 0} if given else {},
        compiler_params=pltpu.CompilerParams(vmem_limit_bytes=60 * 2**20),
        cost_estimate=pl.CostEstimate(
            flops=slab.size, bytes_accessed=5 * slab.size, transcendentals=0
        ),
        name="add_slab",
    )(slab, new, *given)


def local(dosages, allele_counts, slab_in):
    groups, own, samples = dosages.shape
    snps = allele_counts.shape[1]
    rows_n = lax.axis_size("x") * lax.axis_size("zl")
    cores = lax.axis_size("core")
    cols_n = lax.axis_size("zh") * lax.axis_size("y") * cores
    devices = rows_n * cols_n
    block_rows = slab_in.shape[0]
    rows = rows_n * block_rows
    width = samples // devices
    factor = 1.0 / math.sqrt(groups * snps)

    device = lax.axis_index(DEVICES)
    core = lax.axis_index("core")
    counts = lax.dynamic_slice(allele_counts, (0, device * own), (groups, own))
    frequency = counts.astype(jnp.float32) / (2.0 * samples)
    centre = 2.0 * frequency
    inverse = 1.0 / jnp.sqrt(2.0 * frequency * (1.0 - frequency))

    head = dosages[:, :, :rows].astype(jnp.float32)
    head = ((head - centre[:, :, None]) * inverse[:, :, None]).astype(jnp.bfloat16)
    height = block_rows // cores // HALVES
    head = head.reshape(groups * own, rows_n, cores, HALVES, height).transpose(2, 0, 3, 1, 4)
    head = jnp.concatenate(
        [head[:, :, h, b0:b1].reshape(cores, groups * own, -1) for h, b0, b1 in PARTS], axis=2
    )
    head = lax.all_to_all(head, "core", split_axis=0, concat_axis=0, tiled=True)
    head = head.reshape(cores * groups * own, rows // cores)
    sizes = [height * (b1 - b0) for _, b0, b1 in PARTS]
    held = gather_rows(head, [sum(sizes[:i]) for i in range(len(sizes) + 1)])

    columns = spread_columns(dosages, centre, inverse, rows_n, cols_n, width)
    columns = columns.reshape(devices, groups * own, width)
    mine = lax.all_to_all(columns, DEVICES, split_axis=0, concat_axis=0, tiled=True)
    mine = mine.reshape(devices // cores, cores * groups * own, width)
    other = lax.ppermute(mine, "core", [(0, 1), (1, 0)])

    chips = jnp.stack([chips_order(order) for order in ORDERS]).astype(jnp.int32)
    chips = mark(chips)
    out = None
    for half in range(HALVES):
        parts = [i for i, part in enumerate(PARTS) if part[0] == half]
        pieces = [held[i] for i in parts]
        if half == 0:
            product = multiply(pieces, parts, [mine], [core], chips, factor, height)
            product = multiply(pieces, parts, [other], [1 - core], chips, factor, height, product)
        else:
            product = multiply(
                pieces, parts, [mine, other], [core, 1 - core], chips, factor, height
            )
        product = product.reshape(rows_n * cores, height, width)
        product = lax.all_to_all(product, ("x", "zl", "core"), 0, 0, tiled=True)
        product = product.reshape(rows_n, cores, height, width)
        out = add(slab_in, product, half, out)
    return out


def solution(mesh):
    fine = Mesh(mesh.devices.reshape(4, 2, 2, 4, 2), DEVICES)
    row, col = ("x", "zl"), ("zh", "y", "core")

    return jax.shard_map(
        local,
        mesh=fine,
        in_specs=(P(None, row + col, None), P(), P(row, col)),
        out_specs=P(row, col),
        check_vma=False,
    )
```

time: 870 us -> 263 us (0.30)
  waiting for transfers between devices: 752 us -> 97.4 us
  starting transfers between devices: 29.8 us -> 90.2 us
  Pallas kernels: 0 us -> 53.3 us
  matrix products: 50.4 us -> 0 us
  between operations: 15.2 us -> 0.23 us
    all_gather x4 -> x0, waiting for transfers between devices: 535 us -> none  [local(): lax.all_gather(standardized, 'row', axis=1, tiled=True)]
    psum x1 -> x0, waiting for transfers between devices: 159 us -> none  [broadcast(): return lax.psum(kept, axis)]
    ppermute x0 -> x22, waiting for transfers between devices: none -> 68.7 us  [the longest x21 68.7 us: turn(): return lax.ppermute(block, axes + ('core',), pairs)]
    ppermute x0 -> x22, starting transfers between devices: none -> 54.9 us  [the longest x21 54.9 us: turn(): return lax.ppermute(block, axes + ('core',), pairs)]
    pallas_call x0 -> x7, Pallas kernels: none -> 53.3 us  [the longest x3 37.7 us: multiply(): pl.pallas_call(functools.partial(multiply_kernel, scale, starts, parts, c...]
    dot_general x4 -> x0, matrix products: 50.4 us -> none  [local(): lax.dot_general(row_block, lax.all_gather(standardized, 'row', axis=1, ti...]
    all_to_all x4, waiting for transfers between devices: 56.1 us -> 28.7 us  [the longest x2 28.7 us: local(): product = lax.all_to_all(product, ('x', 'zl', 'core'), 0, 0, tiled=True)]
  transfers between devices with their start and end apart: 9 -> 26, of which waited for: 9 -> 13; matrix products, arithmetic and copies ran while one was open for 5% -> 4% of each run, Pallas kernels for 0% -> 19%
where the time goes in v1:
time: 263 us; the launch traced here: 259 us
  waiting for transfers between devices  97.4 us (37%)
  starting transfers between devices  90.2 us (34%)
  Pallas kernels  53.3 us (20%)
  local copies, waits for them, and re-layouts  13.2 us (5%)
  other arithmetic  5.03 us (2%)
    ppermute x21, waiting for transfers between devices, turn(): return lax.ppermute(block, axes + ('core',), pairs)  68.7 us
    ppermute x21, starting transfers between devices, turn(): return lax.ppermute(block, axes + ('core',), pairs)  54.9 us
    pallas_call x3, Pallas kernels, multiply(): pl.pallas_call(functools.partial(multiply_kernel, scale, starts, parts, c...  37.7 us
    all_to_all x2, waiting for transfers between devices, local(): product = lax.all_to_all(product, ('x', 'zl', 'core'), 0, 0, tiled=True)  28.7 us
    all_to_all x2, starting transfers between devices, local(): product = lax.all_to_all(product, ('x', 'zl', 'core'), 0, 0, tiled=True)  20.5 us
    all_to_all x1, starting transfers between devices, local(): lax.all_to_all(columns, DEVICES, split_axis=0, concat_axis=0, tiled=True)  10.7 us
    pallas_call x2, Pallas kernels, add(): pl.pallas_call(add_kernel, grid=(cores,), in_specs=[pl.BlockSpec((height,...  8.58 us
    unnamed x18, local copies, waits for them, and re-layouts  7.05 us
  transfers between devices with their start and end apart: 26, of which 13 were waited for; matrix products, arithmetic and copies ran while one was open for 4% of the time, Pallas kernels for 19%

profile of v1, /device:TPU:5, one launch (start us, length us, event | category | flops | bytes accessed | tf_op | source)
XLA Modules:
  0.0 259.3 jit_solution(2011842613030137634)
XLA Ops:
  3.5 4.1 %all-to-all-start = ((bf16[2,32,2048]{2,1,0:T(8,128)(2,1)}), bf16[2,32,2048]{2,1,0:T(8,128)(2,1)S(1)}, u32[]{:S(2)}, u32[]{:S(2)}) async-start(bf16[2,32,2048]{2,1,0:T(8,128)(2,1)} %pad_maximum_fusion.1), calls=%async_computation | async-start | bytes 524288 | tf_op jit(solution)/shard_map/all_to_all | solution.py:248
  9.0 5.7 %spread_columns.1 = bf16[8,16,32,512]{3,2,1,0:T(8,128)(2,1)} custom-call(bf16[4,8,65536]{2,1,0:T(8,128)(2,1)} %dosages.1, f32[32,1]{1,0:T(8,128)} %reshape.364.centre, f32[32,1]{1,0:T(8,128)} %reshape.365.inverse), custom_call_target="tpu_custom_call" | custom-call | flops 8388608 | bytes 8388608 | tf_op jit(solution)/shard_map/spread_columns/pallas_call | solution.py:101
  14.7 10.7 %all-to-all-start.1 = ((bf16[128,32,512]{2,1,0:T(8,128)(2,1)}), bf16[128,32,512]{2,1,0:T(8,128)(2,1)}, u32[]{:S(2)}, u32[]{:S(2)}) async-start(bf16[128,32,512]{2,1,0:T(8,128)(2,1)} %bitcast.30), calls=%async_computation.1 | async-start | bytes 8388608 | tf_op jit(solution)/shard_map/all_to_all | solution.py:255
  27.0 3.2 %collective-permute-start.10 = (bf16[64,512]{1,0:T(8,128)(2,1)S(1)}, bf16[64,512]{1,0:T(8,128)(2,1)S(1)}, u32[]{:S(2)}, u32[]{:S(2)}) collective-permute-start(bf16[64,512]{1,0:T(8,128)(2,1)S(1)} %get-tuple-element.13), channel_id=1, source_target_pairs={{0,16},{1,25},{16,8},{17,1},{8,24},{9,17},{24,0},{25,9},{2,18},{3,... | collective-permute-start | bytes 196616 | tf_op jit(solution)/shard_map/ppermute | solution.py:35
  30.8 15.4 %collective-permute-done.10 = bf16[64,512]{1,0:T(8,128)(2,1)S(1)} collective-permute-done((bf16[64,512]{1,0:T(8,128)(2,1)S(1)}, bf16[64,512]{1,0:T(8,128)(2,1)S(1)}, u32[]{:S(2)}, u32[]{:S(2)}) %collective-permute-start.10) | collective-permute-done | bytes 65568 | tf_op jit(solution)/shard_map/ppermute | solution.py:35
  46.2 26.2 %collective-permute-start.12 = (bf16[64,512]{1,0:T(8,128)(2,1)S(1)}, bf16[64,512]{1,0:T(8,128)(2,1)S(1)}, u32[]{:S(2)}, u32[]{:S(2)}) collective-permute-start(bf16[64,512]{1,0:T(8,128)(2,1)S(1)} %collective-permute-done.10), channel_id=1, source_target_pairs={{0,16},{1,25},{16,8},{17,1},{8,24},{9,17},{24,0},{25,9},{2,18},{3,... | collective-permute-start | bytes 196616 | tf_op jit(solution)/shard_map/ppermute | solution.py:35
  72.5 2.6 collective-permute-done
  77.0 2.8 %collective-permute-done.2 = bf16[64,1536]{1,0:T(8,128)(2,1)S(1)} collective-permute-done((bf16[64,1536]{1,0:T(8,128)(2,1)S(1)}, bf16[64,1536]{1,0:T(8,128)(2,1)S(1)}, u32[]{:S(2)}, u32[]{:S(2)}) %collective-permute-start.2) | collective-permute-done | bytes 196640 | tf_op jit(solution)/shard_map/ppermute | solution.py:35
  80.6 3.1 %collective-permute-start.3 = (bf16[256,1024]{1,0:T(8,128)(2,1)S(1)}, bf16[256,1024]{1,0:T(8,128)(2,1)}, u32[]{:S(2)}, u32[]{:S(2)}) collective-permute-start(bf16[256,1024]{1,0:T(8,128)(2,1)S(1)} %pad_maximum_fusion), channel_id=1, source_target_pairs={{0,16},{1,25},{16,8},{17,1},{8,24},{9,17},{24,0},{25,9},{2,18},{3,... | collective-permute-start | bytes 1572872 | tf_op jit(solution)/shard_map/ppermute | solution.py:35
  84.6 2.6 %collective-permute-start.13 = (bf16[256,1024]{1,0:T(8,128)(2,1)}, bf16[256,1024]{1,0:T(8,128)(2,1)S(1)}, u32[]{:S(2)}, u32[]{:S(2)}) collective-permute-start(bf16[256,1024]{1,0:T(8,128)(2,1)} %maximum_maximum_fusion), channel_id=1, source_target_pairs={{0,2},{1,7},{2,4},{3,1},{4,6},{5,3},{6,0},{7,5},{8,10},{9,15},{10,... | collective-permute-start | bytes 1572872 | tf_op jit(solution)/shard_map/ppermute | solution.py:35
  88.6 2.1 collective-permute-done.3
  90.6 3.4 %collective-permute-start.5 = (bf16[256,1024]{1,0:T(8,128)(2,1)}, bf16[256,1024]{1,0:T(8,128)(2,1)S(1)}, u32[]{:S(2)}, u32[]{:S(2)}) collective-permute-start(bf16[256,1024]{1,0:T(8,128)(2,1)} %collective-permute-done.3), channel_id=1, source_target_pairs={{0,16},{1,25},{16,8},{17,1},{8,24},{9,17},{24,0},{25,9},{2,18},{3,... | collective-permute-start | bytes 1572872 | tf_op jit(solution)/shard_map/ppermute | solution.py:35
  94.0 2.8 %collective-permute-done.13 = bf16[256,1024]{1,0:T(8,128)(2,1)S(1)} collective-permute-done((bf16[256,1024]{1,0:T(8,128)(2,1)}, bf16[256,1024]{1,0:T(8,128)(2,1)S(1)}, u32[]{:S(2)}, u32[]{:S(2)}) %collective-permute-start.13) | collective-permute-done | bytes 524320 | tf_op jit(solution)/shard_map/ppermute | solution.py:35
  96.9 3.3 %collective-permute-start.15 = (bf16[256,1024]{1,0:T(8,128)(2,1)S(1)}, bf16[256,1024]{1,0:T(8,128)(2,1)S(1)}, u32[]{:S(2)}, u32[]{:S(2)}) collective-permute-start(bf16[256,1024]{1,0:T(8,128)(2,1)S(1)} %collective-permute-done.13), channel_id=1, source_target_pairs={{0,2},{1,7},{2,4},{3,1},{4,6},{5,3},{6,0},{7,5},{8,10},{9,15},{10,... | collective-permute-start | bytes 1572872 | tf_op jit(solution)/shard_map/ppermute | solution.py:35
  100.2 1.9 constant_dynamic-update-slice_fusion.2
  103.0 3.3 %collective-permute-done.15 = bf16[256,1024]{1,0:T(8,128)(2,1)S(1)} collective-permute-done((bf16[256,1024]{1,0:T(8,128)(2,1)S(1)}, bf16[256,1024]{1,0:T(8,128)(2,1)S(1)}, u32[]{:S(2)}, u32[]{:S(2)}) %collective-permute-start.15) | collective-permute-done | bytes 524320 | tf_op jit(solution)/shard_map/ppermute | solution.py:35
  107.3 3.1 %collective-permute-start.6 = (bf16[1024,1024]{1,0:T(8,128)(2,1)}, bf16[1024,1024]{1,0:T(8,128)(2,1)}, u32[]{:S(2)}, u32[]{:S(2)}) collective-permute-start(bf16[1024,1024]{1,0:T(8,128)(2,1)} %constant_dynamic-update-slice_fusion.refs_0_), channel_id=1, source_target_pairs={{0,2},{1,7},{2,4},{3,1},{4,6},{5,3},{6,0},{7,5},{8,10},{9,15},{10,... | collective-permute-start | bytes 6291464 | tf_op jit(solution)/shard_map/ppermute | solution.py:35
  112.0 13.9 %collective-permute-done.16.refs_1_ = bf16[1024,512]{1,0:T(8,128)(2,1)S(1)} collective-permute-done((bf16[1024,512]{1,0:T(8,128)(2,1)S(1)}, bf16[1024,512]{1,0:T(8,128)(2,1)S(1)}, u32[]{:S(2)}, u32[]{:S(2)}) %collective-permute-start.16) | collective-permute-done | bytes 1048608 | tf_op jit(solution)/shard_map/ppermute | solution.py:35
  125.8 9.5 %collective-permute-done.17.refs_2_ = bf16[1024,512]{1,0:T(8,128)(2,1)S(1)} collective-permute-done((bf16[1024,512]{1,0:T(8,128)(2,1)S(1)}, bf16[1024,512]{1,0:T(8,128)(2,1)S(1)}, u32[]{:S(2)}, u32[]{:S(2)}) %collective-permute-start.17) | collective-permute-done | bytes 1048608 | tf_op jit(solution)/shard_map/ppermute | solution.py:35
  137.7 2.1 collective-permute-done.20.refs_6_
  139.9 3.8 %collective-permute-start.8 = (bf16[1024,1024]{1,0:T(8,128)(2,1)}, bf16[1024,1024]{1,0:T(8,128)(2,1)}, u32[]{:S(2)}, u32[]{:S(2)}) collective-permute-start(bf16[1024,1024]{1,0:T(8,128)(2,1)} %collective-permute-done.6.refs_1_), channel_id=1, source_target_pairs={{0,2},{1,7},{2,4},{3,1},{4,6},{5,3},{6,0},{7,5},{8,10},{9,15},{10,... | collective-permute-start | bytes 6291464 | tf_op jit(solution)/shard_map/ppermute | solution.py:35
  146.0 4.4 %collective-permute-done.18.refs_3_ = bf16[1024,512]{1,0:T(8,128)(2,1)} collective-permute-done((bf16[1024,512]{1,0:T(8,128)(2,1)S(1)}, bf16[1024,512]{1,0:T(8,128)(2,1)}, u32[]{:S(2)}, u32[]{:S(2)}) %collective-permute-start.18) | collective-permute-done | bytes 1048608 | tf_op jit(solution)/shard_map/ppermute | solution.py:35
  150.4 9.6 %collective-permute-done.21.refs_7_ = bf16[1024,512]{1,0:T(8,128)(2,1)} collective-permute-done((bf16[1024,512]{1,0:T(8,128)(2,1)}, bf16[1024,512]{1,0:T(8,128)(2,1)}, u32[]{:S(2)}, u32[]{:S(2)}) %collective-permute-start.21) | collective-permute-done | bytes 1048608 | tf_op jit(solution)/shard_map/ppermute | solution.py:35
  161.9 10.7 %multiply.8.refs_9_ = bf16[8,2,128,512]{3,2,1,0:T(8,128)(2,1)} custom-call(s32[1]{0:T(128)} %bitcast.slots, s32[3,64]{1,0:T(4,128)S(1)} %copy-done.3, bf16[1024,512]{1,0:T(8,128)(2,1)S(1)} %get-tuple-element.6.refs_0_, bf16[1024,512]{1,0:T(8,128)(2,1)S(1)} %collective-permute-done.16.refs_1_, bf16[1024,512]{1,0:T(8,128)(2,1)S(1)} %copy-done.1, ...), custom_call_target="tpu_custom_call" | custom-call | flops 4294967296 | bytes 13631488 | tf_op jit(solution)/shard_map/multiply/pallas_call | solution.py:165
  172.6 10.7 %multiply.9 = bf16[8,2,128,512]{3,2,1,0:T(8,128)(2,1)} custom-call(s32[1]{0:T(128)} %bitcast.1.slots, s32[3,64]{1,0:T(4,128)S(1)} %copy-done.3, bf16[1024,512]{1,0:T(8,128)(2,1)S(1)} %get-tuple-element.6.refs_0_, bf16[1024,512]{1,0:T(8,128)(2,1)S(1)} %collective-permute-done.16.refs_1_, ...), custom_call_target="tpu_custom_call", output_to_operand_aliasing={{}: (11, {})} | custom-call | flops 4294967296 | bytes 13631488 | tf_op jit(solution)/shard_map/multiply/pallas_call | solution.py:165
  183.4 12.7 %all-to-all-start.3 = ((bf16[16,128,512]{2,1,0:T(8,128)(2,1)}), bf16[16,128,512]{2,1,0:T(8,128)(2,1)}, u32[]{:S(2)}, u32[]{:S(2)}) async-start(bf16[16,128,512]{2,1,0:T(8,128)(2,1)} %bitcast.31), calls=%async_computation.3 | async-start | bytes 4194304 | tf_op jit(solution)/shard_map/all_to_all | solution.py:273
  196.7 16.3 %multiply.7 = bf16[8,2,128,512]{3,2,1,0:T(8,128)(2,1)} custom-call(s32[2]{0:T(128)} %pad_add_fusion.1.slots, s32[3,64]{1,0:T(4,128)} %mark.1.chips, bf16[1024,1024]{1,0:T(8,128)(2,1)} %constant_dynamic-update-slice_fusion.refs_0_, bf16[1024,1024]{1,0:T(8,128)(2,1)} %collective-permute-done.6.refs_1_, bf16[1024,1024]{1,0:T(8,128)(2,1)} %collective-permute-done.7.refs_2_, ...), custom_call_target="tpu_custom_call" | custom-call | flops 8589934592 | bytes 18874368 | tf_op jit(solution)/shard_map/multiply/pallas_call | solution.py:165
  213.0 8.1 %all-to-all-done.3 = bf16[16,128,512]{2,1,0:T(8,128)(2,1)} async-done(((bf16[16,128,512]{2,1,0:T(8,128)(2,1)}), bf16[16,128,512]{2,1,0:T(8,128)(2,1)}, u32[]{:S(2)}, u32[]{:S(2)}) %all-to-all-start.3) | async-done | bytes 2097184 | tf_op jit(solution)/shard_map/all_to_all | solution.py:273
  221.1 7.8 %all-to-all-start.2 = ((bf16[16,128,512]{2,1,0:T(8,128)(2,1)}), bf16[16,128,512]{2,1,0:T(8,128)(2,1)S(1)}, u32[]{:S(2)}, u32[]{:S(2)}) async-start(bf16[16,128,512]{2,1,0:T(8,128)(2,1)} %bitcast.35), calls=%async_computation.2 | async-start | bytes 4194304 | tf_op jit(solution)/shard_map/all_to_all | solution.py:273
  228.8 4.3 %add_slab.2.refs_0_ = f32[512,4096]{1,0:T(8,128)} custom-call(f32[512,4096]{1,0:T(8,128)} %slab.3, bf16[8,2,128,512]{3,2,1,0:T(8,128)(2,1)} %bitcast.21.new), custom_call_target="tpu_custom_call" | custom-call | flops 2097152 | bytes 10485760 | tf_op jit(solution)/shard_map/add_slab/pallas_call | solution.py:203
  233.1 20.6 %all-to-all-done.2 = bf16[16,128,512]{2,1,0:T(8,128)(2,1)S(1)} async-done(((bf16[16,128,512]{2,1,0:T(8,128)(2,1)}), bf16[16,128,512]{2,1,0:T(8,128)(2,1)S(1)}, u32[]{:S(2)}, u32[]{:S(2)}) %all-to-all-start.2) | async-done | bytes 2097184 | tf_op jit(solution)/shard_map/all_to_all | solution.py:273
  255.0 4.3 %add_slab.3 = f32[512,4096]{1,0:T(8,128)} custom-call(f32[512,4096]{1,0:T(8,128)} %slab.3, bf16[8,2,128,512]{3,2,1,0:T(8,128)(2,1)} %bitcast.32, f32[512,4096]{1,0:T(8,128)} %add_slab.2.refs_0_), custom_call_target="tpu_custom_call", output_to_operand_aliasing={{}: (2, {})} | custom-call | flops 2097152 | bytes 10485760 | tf_op jit(solution)/shard_map/add_slab/pallas_call | solution.py:203
  (81 shorter events, 23.8 us)
Async XLA Ops:
  3.5 11.2 %all-to-all-start = ((bf16[2,32,2048]{2,1,0:T(8,128)(2,1)}), bf16[2,32,2048]{2,1,0:T(8,128)(2,1)S(1)}, u32[]{:S(2)}, u32[]{:S(2)}) async-start(bf16[2,32,2048]{2,1,0:T(8,128)(2,1)} %pad_maximum_fusion.1), calls=%async_computation | async-start | bytes 524288 | tf_op jit(solution)/shard_map/all_to_all | solution.py:248
  14.7 72.5 %all-to-all-start.1 = ((bf16[128,32,512]{2,1,0:T(8,128)(2,1)}), bf16[128,32,512]{2,1,0:T(8,128)(2,1)}, u32[]{:S(2)}, u32[]{:S(2)}) async-start(bf16[128,32,512]{2,1,0:T(8,128)(2,1)} %bitcast.30), calls=%async_computation.1 | async-start | bytes 8388608 | tf_op jit(solution)/shard_map/all_to_all | solution.py:255
  25.4 49.7 %collective-permute-start = (bf16[64,1536]{1,0:T(8,128)(2,1)S(1)}, bf16[64,1536]{1,0:T(8,128)(2,1)S(1)}, u32[]{:S(2)}, u32[]{:S(2)}) collective-permute-start(bf16[64,1536]{1,0:T(8,128)(2,1)S(1)} %slice.86), channel_id=1, source_target_pairs={{0,32},{1,97},{32,64},{33,1},{64,96},{65,33},{96,0},{97,65},{2,34}... | collective-permute-start | bytes 589832 | tf_op jit(solution)/shard_map/ppermute | solution.py:35
  25.7 50.6 %collective-permute-start.1 = (bf16[64,1536]{1,0:T(8,128)(2,1)S(1)}, bf16[64,1536]{1,0:T(8,128)(2,1)S(1)}, u32[]{:S(2)}, u32[]{:S(2)}) collective-permute-start(bf16[64,1536]{1,0:T(8,128)(2,1)S(1)} %slice.86), channel_id=1, source_target_pairs={{0,96},{1,33},{32,0},{33,65},{64,32},{65,97},{96,64},{97,1},{2,98}... | collective-permute-start | bytes 589832 | tf_op jit(solution)/shard_map/ppermute | solution.py:35
  27.0 19.3 %collective-permute-start.10 = (bf16[64,512]{1,0:T(8,128)(2,1)S(1)}, bf16[64,512]{1,0:T(8,128)(2,1)S(1)}, u32[]{:S(2)}, u32[]{:S(2)}) collective-permute-start(bf16[64,512]{1,0:T(8,128)(2,1)S(1)} %get-tuple-element.13), channel_id=1, source_target_pairs={{0,16},{1,25},{16,8},{17,1},{8,24},{9,17},{24,0},{25,9},{2,18},{3,... | collective-permute-start | bytes 196616 | tf_op jit(solution)/shard_map/ppermute | solution.py:35
  30.1 53.6 %collective-permute-start.11 = (bf16[64,512]{1,0:T(8,128)(2,1)S(1)}, bf16[64,512]{1,0:T(8,128)(2,1)S(1)}, u32[]{:S(2)}, u32[]{:S(2)}) collective-permute-start(bf16[64,512]{1,0:T(8,128)(2,1)S(1)} %get-tuple-element.13), channel_id=1, source_target_pairs={{0,24},{1,17},{16,0},{17,9},{8,16},{9,25},{24,8},{25,1},{2,26},{3,... | collective-permute-start | bytes 196616 | tf_op jit(solution)/shard_map/ppermute | solution.py:35
  46.2 37.5 %collective-permute-start.12 = (bf16[64,512]{1,0:T(8,128)(2,1)S(1)}, bf16[64,512]{1,0:T(8,128)(2,1)S(1)}, u32[]{:S(2)}, u32[]{:S(2)}) collective-permute-start(bf16[64,512]{1,0:T(8,128)(2,1)S(1)} %collective-permute-done.10), channel_id=1, source_target_pairs={{0,16},{1,25},{16,8},{17,1},{8,24},{9,17},{24,0},{25,9},{2,18},{3,... | collective-permute-start | bytes 196616 | tf_op jit(solution)/shard_map/ppermute | solution.py:35
  75.1 4.8 %collective-permute-start.2 = (bf16[64,1536]{1,0:T(8,128)(2,1)S(1)}, bf16[64,1536]{1,0:T(8,128)(2,1)S(1)}, u32[]{:S(2)}, u32[]{:S(2)}) collective-permute-start(bf16[64,1536]{1,0:T(8,128)(2,1)S(1)} %collective-permute-done), channel_id=1, source_target_pairs={{0,32},{1,97},{32,64},{33,1},{64,96},{65,33},{96,0},{97,65},{2,34}... | collective-permute-start | bytes 589832 | tf_op jit(solution)/shard_map/ppermute | solution.py:35
  80.6 10.0 %collective-permute-start.3 = (bf16[256,1024]{1,0:T(8,128)(2,1)S(1)}, bf16[256,1024]{1,0:T(8,128)(2,1)}, u32[]{:S(2)}, u32[]{:S(2)}) collective-permute-start(bf16[256,1024]{1,0:T(8,128)(2,1)S(1)} %pad_maximum_fusion), channel_id=1, source_target_pairs={{0,16},{1,25},{16,8},{17,1},{8,24},{9,17},{24,0},{25,9},{2,18},{3,... | collective-permute-start | bytes 1572872 | tf_op jit(solution)/shard_map/ppermute | solution.py:35
  84.6 12.3 %collective-permute-start.13 = (bf16[256,1024]{1,0:T(8,128)(2,1)}, bf16[256,1024]{1,0:T(8,128)(2,1)S(1)}, u32[]{:S(2)}, u32[]{:S(2)}) collective-permute-start(bf16[256,1024]{1,0:T(8,128)(2,1)} %maximum_maximum_fusion), channel_id=1, source_target_pairs={{0,2},{1,7},{2,4},{3,1},{4,6},{5,3},{6,0},{7,5},{8,10},{9,15},{10,... | collective-permute-start | bytes 1572872 | tf_op jit(solution)/shard_map/ppermute | solution.py:35
  87.2 85.4 %collective-permute-start.9 = (bf16[64,64,512]{2,1,0:T(8,128)(2,1)}, bf16[64,64,512]{2,1,0:T(8,128)(2,1)}, u32[]{:S(2)}, u32[]{:S(2)}) collective-permute-start(bf16[64,64,512]{2,1,0:T(8,128)(2,1)} %bitcast.17.refs_4_.refs_8_), channel_id=1, source_target_pairs={{0,1},{1,0},{2,3},{3,2},{4,5},{5,4},{6,7},{7,6},{8,9},{9,8},{10,11... | collective-permute-start | bytes 12582920 | tf_op jit(solution)/shard_map/ppermute | solution.py:257
  87.2 14.9 %collective-permute-start.4 = (bf16[256,1024]{1,0:T(8,128)(2,1)S(1)}, bf16[256,1024]{1,0:T(8,128)(2,1)S(1)}, u32[]{:S(2)}, u32[]{:S(2)}) collective-permute-start(bf16[256,1024]{1,0:T(8,128)(2,1)S(1)} %pad_maximum_fusion), channel_id=1, source_target_pairs={{0,24},{1,17},{16,0},{17,9},{8,16},{9,25},{24,8},{25,1},{2,26},{3,... | collective-permute-start | bytes 1572872 | tf_op jit(solution)/shard_map/ppermute | solution.py:35
  87.3 15.6 %collective-permute-start.14 = (bf16[256,1024]{1,0:T(8,128)(2,1)}, bf16[256,1024]{1,0:T(8,128)(2,1)S(1)}, u32[]{:S(2)}, u32[]{:S(2)}) collective-permute-start(bf16[256,1024]{1,0:T(8,128)(2,1)} %maximum_maximum_fusion), channel_id=1, source_target_pairs={{0,6},{1,3},{2,0},{3,5},{4,2},{5,7},{6,4},{7,1},{8,14},{9,11},{10,... | collective-permute-start | bytes 1572872 | tf_op jit(solution)/shard_map/ppermute | solution.py:35
  90.6 15.8 %collective-permute-start.5 = (bf16[256,1024]{1,0:T(8,128)(2,1)}, bf16[256,1024]{1,0:T(8,128)(2,1)S(1)}, u32[]{:S(2)}, u32[]{:S(2)}) collective-permute-start(bf16[256,1024]{1,0:T(8,128)(2,1)} %collective-permute-done.3), channel_id=1, source_target_pairs={{0,16},{1,25},{16,8},{17,1},{8,24},{9,17},{24,0},{25,9},{2,18},{3,... | collective-permute-start | bytes 1572872 | tf_op jit(solution)/shard_map/ppermute | solution.py:35
  96.9 9.4 %collective-permute-start.15 = (bf16[256,1024]{1,0:T(8,128)(2,1)S(1)}, bf16[256,1024]{1,0:T(8,128)(2,1)S(1)}, u32[]{:S(2)}, u32[]{:S(2)}) collective-permute-start(bf16[256,1024]{1,0:T(8,128)(2,1)S(1)} %collective-permute-done.13), channel_id=1, source_target_pairs={{0,2},{1,7},{2,4},{3,1},{4,6},{5,3},{6,0},{7,5},{8,10},{9,15},{10,... | collective-permute-start | bytes 1572872 | tf_op jit(solution)/shard_map/ppermute | solution.py:35
  106.3 19.5 %collective-permute-start.16 = (bf16[1024,512]{1,0:T(8,128)(2,1)S(1)}, bf16[1024,512]{1,0:T(8,128)(2,1)S(1)}, u32[]{:S(2)}, u32[]{:S(2)}) collective-permute-start(bf16[1024,512]{1,0:T(8,128)(2,1)S(1)} %get-tuple-element.6.refs_0_), channel_id=1, source_target_pairs={{0,16},{1,25},{16,8},{17,1},{8,24},{9,17},{24,0},{25,9},{2,18},{3,... | collective-permute-start | bytes 3145736 | tf_op jit(solution)/shard_map/ppermute | solution.py:35
  107.3 32.6 %collective-permute-start.6 = (bf16[1024,1024]{1,0:T(8,128)(2,1)}, bf16[1024,1024]{1,0:T(8,128)(2,1)}, u32[]{:S(2)}, u32[]{:S(2)}) collective-permute-start(bf16[1024,1024]{1,0:T(8,128)(2,1)} %constant_dynamic-update-slice_fusion.refs_0_), channel_id=1, source_target_pairs={{0,2},{1,7},{2,4},{3,1},{4,6},{5,3},{6,0},{7,5},{8,10},{9,15},{10,... | collective-permute-start | bytes 6291464 | tf_op jit(solution)/shard_map/ppermute | solution.py:35
  110.4 25.0 %collective-permute-start.17 = (bf16[1024,512]{1,0:T(8,128)(2,1)S(1)}, bf16[1024,512]{1,0:T(8,128)(2,1)S(1)}, u32[]{:S(2)}, u32[]{:S(2)}) collective-permute-start(bf16[1024,512]{1,0:T(8,128)(2,1)S(1)} %get-tuple-element.6.refs_0_), channel_id=1, source_target_pairs={{0,24},{1,17},{16,0},{17,9},{8,16},{9,25},{24,8},{25,1},{2,26},{3,... | collective-permute-start | bytes 3145736 | tf_op jit(solution)/shard_map/ppermute | solution.py:35
  111.8 24.5 %collective-permute-start.19 = (bf16[1024,512]{1,0:T(8,128)(2,1)S(1)}, bf16[1024,512]{1,0:T(8,128)(2,1)}, u32[]{:S(2)}, u32[]{:S(2)}) collective-permute-start(bf16[1024,512]{1,0:T(8,128)(2,1)S(1)} %get-tuple-element.5.refs_4_), channel_id=1, source_target_pairs={{0,32},{1,97},{32,64},{33,1},{64,96},{65,33},{96,0},{97,65},{2,34}... | collective-permute-start | bytes 3145736 | tf_op jit(solution)/shard_map/ppermute | solution.py:35
  125.8 14.0 %collective-permute-start.20 = (bf16[1024,512]{1,0:T(8,128)(2,1)S(1)}, bf16[1024,512]{1,0:T(8,128)(2,1)}, u32[]{:S(2)}, u32[]{:S(2)}) collective-permute-start(bf16[1024,512]{1,0:T(8,128)(2,1)S(1)} %get-tuple-element.5.refs_4_), channel_id=1, source_target_pairs={{0,96},{1,33},{32,0},{33,65},{64,32},{65,97},{96,64},{97,1},{2,98}... | collective-permute-start | bytes 3145736 | tf_op jit(solution)/shard_map/ppermute | solution.py:35
  135.3 1.0 copy-start
  136.3 14.0 %collective-permute-start.18 = (bf16[1024,512]{1,0:T(8,128)(2,1)S(1)}, bf16[1024,512]{1,0:T(8,128)(2,1)}, u32[]{:S(2)}, u32[]{:S(2)}) collective-permute-start(bf16[1024,512]{1,0:T(8,128)(2,1)S(1)} %collective-permute-done.16.refs_1_), channel_id=1, source_target_pairs={{0,16},{1,25},{16,8},{17,1},{8,24},{9,17},{24,0},{25,9},{2,18},{3,... | collective-permute-start | bytes 3145736 | tf_op jit(solution)/shard_map/ppermute | solution.py:35
  136.3 23.6 %collective-permute-start.21 = (bf16[1024,512]{1,0:T(8,128)(2,1)}, bf16[1024,512]{1,0:T(8,128)(2,1)}, u32[]{:S(2)}, u32[]{:S(2)}) collective-permute-start(bf16[1024,512]{1,0:T(8,128)(2,1)} %collective-permute-done.19.refs_5_), channel_id=1, source_target_pairs={{0,32},{1,97},{32,64},{33,1},{64,96},{65,33},{96,0},{97,65},{2,34}... | collective-permute-start | bytes 3145736 | tf_op jit(solution)/shard_map/ppermute | solution.py:35
  139.9 56.8 %collective-permute-start.7 = (bf16[1024,1024]{1,0:T(8,128)(2,1)}, bf16[1024,1024]{1,0:T(8,128)(2,1)}, u32[]{:S(2)}, u32[]{:S(2)}) collective-permute-start(bf16[1024,1024]{1,0:T(8,128)(2,1)} %constant_dynamic-update-slice_fusion.refs_0_), channel_id=1, source_target_pairs={{0,6},{1,3},{2,0},{3,5},{4,2},{5,7},{6,4},{7,1},{8,14},{9,11},{10,... | collective-permute-start | bytes 6291464 | tf_op jit(solution)/shard_map/ppermute | solution.py:35
  139.9 56.8 %collective-permute-start.8 = (bf16[1024,1024]{1,0:T(8,128)(2,1)}, bf16[1024,1024]{1,0:T(8,128)(2,1)}, u32[]{:S(2)}, u32[]{:S(2)}) collective-permute-start(bf16[1024,1024]{1,0:T(8,128)(2,1)} %collective-permute-done.6.refs_1_), channel_id=1, source_target_pairs={{0,2},{1,7},{2,4},{3,1},{4,6},{5,3},{6,0},{7,5},{8,10},{9,15},{10,... | collective-permute-start | bytes 6291464 | tf_op jit(solution)/shard_map/ppermute | solution.py:35
  160.0 1.2 copy-start.1
  161.2 0.7 copy-start.3
  161.9 10.7 %copy-start.2 = (bf16[1024,512]{1,0:T(8,128)(2,1)S(1)}, bf16[1024,512]{1,0:T(8,128)(2,1)}, u32[]{:S(2)}) copy-start(bf16[1024,512]{1,0:T(8,128)(2,1)} %copy-done) | copy-start | bytes 3145732
  183.4 37.7 %all-to-all-start.3 = ((bf16[16,128,512]{2,1,0:T(8,128)(2,1)}), bf16[16,128,512]{2,1,0:T(8,128)(2,1)}, u32[]{:S(2)}, u32[]{:S(2)}) async-start(bf16[16,128,512]{2,1,0:T(8,128)(2,1)} %bitcast.31), calls=%async_computation.3 | async-start | bytes 4194304 | tf_op jit(solution)/shard_map/all_to_all | solution.py:273
  221.1 32.6 %all-to-all-start.2 = ((bf16[16,128,512]{2,1,0:T(8,128)(2,1)}), bf16[16,128,512]{2,1,0:T(8,128)(2,1)S(1)}, u32[]{:S(2)}, u32[]{:S(2)}) async-start(bf16[16,128,512]{2,1,0:T(8,128)(2,1)} %bitcast.35), calls=%async_computation.2 | async-start | bytes 4194304 | tf_op jit(solution)/shard_map/all_to_all | solution.py:273
  253.7 1.3 copy-start.4
